TPU v7x, 32 devices: a whole 2x2x4 slice. The times are simulated.
32 devices in a mesh: dp: 2 (over x), col: 4 (over z), row: 4 (over y, core).
Axes of the slice: x: 2, y: 2, z: 4, core: 2. Of those that a mesh axis runs over, the one named last changes fastest.
Arguments:
- hidden: bfloat16 [256, 3584], P('dp', 'row'), parts along dimension 0
- mrope_ids: int32 [3, 256], P(None, ('dp', 'row')), parts along dimension 1
- cache_lens: int32 [256], P(('dp', 'row')), parts along dimension 0
- k_cache: bfloat16 [256, 1024, 4, 128], P(('dp', 'row'), None, 'col'), parts along dimension 0
- v_cache: bfloat16 [256, 1024, 4, 128], P(('dp', 'row'), None, 'col'), parts along dimension 0
- norm_attn: bfloat16 [3584], P('row')
- w_qkv: bfloat16 [3584, 4608], P('row', 'col')
- b_qkv: bfloat16 [4608], P('col')
- w_out: bfloat16 [3584, 3584], P('col', 'row')
- norm_mlp: bfloat16 [3584], P('row')
- w_gate: bfloat16 [3584, 18944], P('row', 'col')
- w_up: bfloat16 [3584, 18944], P('row', 'col')
- w_down: bfloat16 [18944, 3584], P('col', 'row')
Outputs:
- output 1: bfloat16 [256, 3584], P('dp', 'row'), parts along dimension 0
- output 2: bfloat16 [256, 1024, 4, 128], P(('dp', 'row'), None, 'col'), parts along dimension 0
- output 3: bfloat16 [256, 1024, 4, 128], P(('dp', 'row'), None, 'col'), parts along dimension 0
There are 2 independent parts. A program takes and returns all parts, laid end to end along the dimension named above; an argument that names none is the same for every part.
All inputs are finite; a program needn't handle non-finite values.
Results may differ from a plain program's by a relative error of at most 0.0153839.
Values are sent between devices in bfloat16 or wider.
A program may use at most 1 GiB of HBM per device.

v0:
```python
import functools

import jax
import jax.numpy as jnp
import numpy as np
from jax import lax
from jax.experimental import pallas as pl
from jax.experimental.pallas import tpu as pltpu
from jax.sharding import PartitionSpec as P

MESH = pl.DeviceIdType.MESH
LANES = 128
HEAD_DIM = 128
ROPE_THETA = 1000000.0
NORM_EPS = 1e-6
DOWNSCALE = 2.0 ** -10
BIG = 3.3e38
GROUPS = 2
UNROLL = 8
CACHE_PARTS = 8
CHUNKS = (4, 8, 8, 8, 6, 3)
EARLY = 3
SPREAD_AT = 3
F32 = jnp.float32
BF16 = jnp.bfloat16


def row_peers():
    row = lax.axis_index('row')
    core, y = row % 2, row // 2
    return row, y * 2 + 1 - core, (1 - y) * 2 + core, (1 - y) * 2 + 1 - core


def split_square(sq_sum):
    high = sq_sum.astype(BF16)
    high_f = high.astype(F32)
    low = jnp.where(high_f < BIG, sq_sum - high_f, 0.0).astype(BF16)
    return high, low


def local_scale(sq_sum, width):
    return lax.rsqrt(sq_sum / width + NORM_EPS)


def ratio(total, local):
    return jnp.where(local > 0.0, total / local, 0.0)


def remote(src, dst, send_sem, recv_sem, device):
    return pltpu.make_async_remote_copy(src_ref=src, dst_ref=dst, send_sem=send_sem, recv_sem=recv_sem,
                                        device_id=device, device_id_type=MESH)


def rotate(vec, cos_t, sin_t):
    half = HEAD_DIM // 2
    swapped = jnp.concatenate([-vec[:, half:], vec[:, :half]], axis=1)
    return (vec * cos_t + swapped * sin_t).astype(BF16).astype(F32)


def qkv_kernel(h_hbm, g_hbm, w_hbm, b_hbm, ids_hbm, freq_hbm, kc_hbm, vc_hbm, q_ref, k_ref, v_ref, kc_ref, vc_ref,
               h_ref, g_ref, w_ref, b_ref, ids_ref, freq_ref, part, send, recv, table, q_rows,
               send_sem, recv_sem, load_sem, cache_sem):
    row, *peers = row_peers()
    loads = [pltpu.make_async_copy(src, dst, load_sem.at[i]) for i, (src, dst) in enumerate(
        ((h_hbm, h_ref), (g_hbm, g_ref), (w_hbm, w_ref), (b_hbm, b_ref), (ids_hbm, ids_ref), (freq_hbm, freq_ref)))]
    for copy in loads:
        copy.start()
    width = h_ref.shape[1]
    cols = w_ref.shape[1]
    rows = k_ref.shape[0]
    group = cols // HEAD_DIM - 2
    barrier = pltpu.get_barrier_semaphore()
    for peer in peers:
        pl.semaphore_signal(barrier, inc=1, device_id={'row': peer}, device_id_type=MESH)
    cache_copies = []
    for i in range(CACHE_PARTS):
        at = pl.ds(i * (rows // CACHE_PARTS), rows // CACHE_PARTS)
        cache_copies.append(pltpu.make_async_copy(kc_hbm.at[at], kc_ref.at[at], cache_sem.at[0, i]))
        cache_copies.append(pltpu.make_async_copy(vc_hbm.at[at], vc_ref.at[at], cache_sem.at[1, i]))
    for copy in cache_copies:
        copy.start()

    loads[0].wait()
    loads[1].wait()
    hid = h_ref[...].astype(F32)
    sq_sum = jnp.sum(hid * hid, axis=1, keepdims=True)
    scale = local_scale(sq_sum, width) * DOWNSCALE
    normed = (hid * scale * g_ref[...].astype(F32).reshape(1, -1)).astype(BF16)
    loads[2].wait()
    prod = jnp.dot(normed, w_ref[...], preferred_element_type=F32)
    part[:, 0:cols] = prod
    wide = jnp.broadcast_to(sq_sum, (hid.shape[0], LANES))
    part[:, cols:] = wide
    send[:, 0:cols] = prod.astype(BF16)
    high, low = split_square(wide)
    send[:, cols:cols + LANES] = high
    send[:, cols + LANES:] = low
    pl.semaphore_wait(barrier, 3)
    copies = []
    for slot in (2, 1, 0):
        copies.append(remote(send.at[pl.ds(pl.multiple_of(peers[slot] * rows, rows), rows)], recv.at[slot],
                             send_sem.at[slot], recv_sem.at[slot], {'row': peers[slot]}))
        copies[-1].start()

    for copy in loads[3:]:
        copy.wait()
    table[...] = jnp.zeros_like(table)
    table[0:3, 0:rows] = ids_ref[...].astype(F32)
    by_row = table[...].T
    pair = lax.broadcasted_iota(jnp.int32, (rows, HEAD_DIM), 1) % (HEAD_DIM // 2)
    chosen = jnp.where(pair < 16, by_row[0:rows, 0:1], jnp.where(pair < 40, by_row[0:rows, 1:2], by_row[0:rows, 2:3]))
    angles = chosen * freq_ref[...]
    cos_t, sin_t = jnp.cos(angles), jnp.sin(angles)

    for copy in copies:
        copy.wait_recv()
    mine = part[pl.ds(pl.multiple_of(row * rows, rows), rows), :]
    sums = [mine[:, cols:cols + 1]]
    parts = [mine[:, 0:cols]]
    for slot in range(3):
        block = recv[slot].astype(F32)
        sums.append(block[:, cols:cols + 1] + block[:, cols + LANES:cols + LANES + 1])
        parts.append(block[:, 0:cols])
    total = local_scale(sums[0] + sums[1] + sums[2] + sums[3], 4 * width)
    qkv = jnp.zeros((rows, cols), F32)
    for square, block in zip(sums, parts):
        qkv = qkv + block * ratio(total, local_scale(square, width) * DOWNSCALE)
    qkv = (qkv + b_ref[...].astype(F32).reshape(1, -1)).astype(BF16).astype(F32)
    for head in range(group):
        q_rows[pl.ds(head, rows, stride=8), :] = rotate(qkv[:, head * HEAD_DIM:(head + 1) * HEAD_DIM], cos_t, sin_t)
    for head in range(group, 8):
        q_rows[pl.ds(head, rows, stride=8), :] = jnp.zeros((rows, HEAD_DIM), F32)
    q_ref[...] = q_rows[...]
    k_ref[...] = rotate(qkv[:, group * HEAD_DIM:(group + 1) * HEAD_DIM], cos_t, sin_t)
    v_ref[...] = qkv[:, (group + 1) * HEAD_DIM:]
    for copy in copies:
        copy.wait_send()
    for copy in cache_copies:
        copy.wait()


def attention_kernel(group, unroll, lens_ref, q_ref, nk_ref, nv_ref, k_ref, v_ref, o_ref, k_out, v_out,
                     k_patch, v_patch, o_rows, s_buf, out_sem, patch_sem):
    rows, slots = k_ref.shape[0], k_ref.shape[1]
    steps = rows // unroll

    def stores(step):
        at = pl.ds(step * unroll, unroll)
        return (pltpu.make_async_copy(k_ref.at[at], k_out.at[at], out_sem.at[0, step]),
                pltpu.make_async_copy(v_ref.at[at], v_out.at[at], out_sem.at[1, step]))

    def patches(b):
        base = pl.multiple_of((lens_ref[b] // 16) * 16, 16)
        return (pltpu.make_async_copy(k_patch.at[b], k_out.at[b, pl.ds(base, 16)], patch_sem.at[0, b]),
                pltpu.make_async_copy(v_patch.at[b], v_out.at[b, pl.ds(base, 16)], patch_sem.at[1, b]))

    for step in range(steps):
        for copy in stores(step):
            copy.start()

    @pl.loop(0, rows)
    def _(b):
        base = pl.multiple_of((lens_ref[b] // 16) * 16, 16)
        hit = lax.broadcasted_iota(jnp.int32, (16, HEAD_DIM), 0) == lens_ref[b] % 16
        for src, new, patch in ((k_ref, nk_ref, k_patch), (v_ref, nv_ref, v_patch)):
            old = src[b, pl.ds(base, 16), :].astype(F32)
            patch[b] = jnp.where(hit, new[pl.ds(b, 1), :], old).astype(BF16)

    @pl.loop(0, steps)
    def _(step):
        items = [step * unroll + u for u in range(unroll)]
        position = lax.broadcasted_iota(jnp.int32, (8, slots), 1)
        for u, b in enumerate(items):
            query = q_ref[pl.ds(pl.multiple_of(b * 8, 8), 8), :]
            scores = lax.dot_general(query.astype(BF16), k_ref[b], (((1,), (1,)), ((), ())), preferred_element_type=F32)
            fresh = jnp.sum(query * nk_ref[pl.ds(b, 1), :], axis=1, keepdims=True)
            scores = jnp.where(position == lens_ref[b], fresh, scores) * (HEAD_DIM ** -0.5)
            s_buf[u * 8:(u + 1) * 8, :] = jnp.where(position <= lens_ref[b], scores, -1e30)
        scores = s_buf[...]
        weight = jnp.exp(scores - jnp.max(scores, axis=1, keepdims=True))
        s_buf[...] = weight / jnp.sum(weight, axis=1, keepdims=True)
        for u, b in enumerate(items):
            prob = s_buf[u * 8:(u + 1) * 8, :].astype(BF16)
            newest = position == lens_ref[b]
            prob_f = prob.astype(F32)
            fresh = jnp.sum(jnp.where(newest, prob_f, 0.0), axis=1, keepdims=True)
            rest = jnp.where(newest, 0.0, prob_f).astype(BF16)
            o_rows[pl.ds(pl.multiple_of(b * 8, 8), 8), :] = (
                jnp.dot(rest, v_ref[b], preferred_element_type=F32) + fresh * nv_ref[pl.ds(b, 1), :])

    for head in range(group):
        o_ref[:, head * HEAD_DIM:(head + 1) * HEAD_DIM] = o_rows[pl.ds(head, rows, stride=8), :].astype(BF16)

    for step in range(steps):
        for copy in stores(step):
            copy.wait()

        @pl.loop(step * unroll, (step + 1) * unroll)
        def _(b):
            for copy in patches(b):
                copy.start()

    @pl.loop(0, rows)
    def _(b):
        for copy in patches(b):
            copy.wait()


def mlp_kernel(chunks, o_ref, h_hbm, g_hbm, wo_hbm, wg_hbm, wu_hbm, wd_hbm, out_ref,
               hid, g_ref, wo, wgu, wd, o_all, osend, orecv, own, resid, resid_p, z_p, sums_p, coef,
               part, send1, recv1, send2, recv2, acts, acc, dsend, drecv, final,
               h_sem, g_sem, wo_sem, wgu_sem, wd_sem, osem, rs_sem, ag_sem, s1_sem, s2_sem, ay_sem, ac_sem, aw_sem, ds_sem, da_sem):
    row, mate, across, diagonal = row_peers()
    core, y = row % 2, row // 2
    col = lax.axis_index('col')
    zpeers = [(col + step) % 4 for step in (1, 2, 3)]
    n_tiles = wgu.shape[0]
    width = hid.shape[1]
    group_rows = resid.shape[1]
    rows = group_rows // 2
    block = group_rows // 4
    base = [pl.multiple_of(y * group_rows, group_rows), pl.multiple_of((1 - y) * group_rows, group_rows)]
    n_chunks = len(chunks)
    last = n_chunks - 1

    mine = pl.ds(pl.multiple_of(core * rows, rows), rows)
    theirs = pl.ds(pl.multiple_of((1 - core) * rows, rows), rows)
    wo_copy = pltpu.make_async_copy(wo_hbm, wo, wo_sem)
    wo_copy.start()
    h_copy = pltpu.make_async_copy(h_hbm, hid, h_sem)
    h_copy.start()
    g_copy = pltpu.make_async_copy(g_hbm, g_ref, g_sem)
    g_copy.start()

    barrier = pltpu.get_barrier_semaphore()
    for peer in (diagonal, across, mate):
        pl.semaphore_signal(barrier, inc=1, device_id={'row': peer}, device_id_type=MESH)
    for peer in zpeers:
        pl.semaphore_signal(barrier, inc=1, device_id={'col': peer}, device_id_type=MESH)

    def tile_loads(t):
        at = pl.ds(pl.multiple_of(t * LANES, LANES), LANES)
        return (pltpu.make_async_copy(wg_hbm.at[:, at], wgu.at[t, :, pl.ds(0, LANES)], wgu_sem.at[0, t]),
                pltpu.make_async_copy(wu_hbm.at[:, at], wgu.at[t, :, pl.ds(LANES, LANES)], wgu_sem.at[1, t]))

    @pl.loop(0, n_tiles)
    def _(t):
        for copy in tile_loads(t):
            copy.start()

    wd_copies = []
    for k, (first, count) in enumerate(chunks):
        at = pl.ds(first * LANES, count * LANES)
        wd_copies.append(pltpu.make_async_copy(wd_hbm.at[at], wd.at[at], wd_sem.at[k]))
        wd_copies[-1].start()

    started = []

    def start(copy):
        copy.start()
        started.append(copy)
        return copy

    o_all[0, mine, :] = o_ref[...]
    pl.semaphore_wait(barrier, 6)
    gathers = [start(remote(o_ref, o_all.at[g, mine], osem.at[0, i], osem.at[1, i], {'row': peer}))
               for i, g, peer in ((0, 0, mate), (1, 1, across), (2, 1, diagonal))]

    own_rows = pl.ds(pl.multiple_of(col * block, block), block)
    scatters, spreads = {}, {}

    def project(g):
        if g == 0:
            wo_copy.wait()
            gathers[0].wait_recv()
        else:
            gathers[1].wait_recv()
            gathers[2].wait_recv()
        prod = jnp.dot(o_all[g], wo[...], preferred_element_type=F32)
        own[g] = prod
        osend[g] = prod.astype(BF16)
        scatters[g] = [start(remote(osend.at[g, pl.ds(pl.multiple_of(zpeers[i] * block, block), block)], orecv.at[g, i],
                                    rs_sem.at[0, g, i], rs_sem.at[1, g, i], {'col': zpeers[i]})) for i in (1, 2, 0)]

    def spread(g):
        if g == 0:
            h_copy.wait()
            g_copy.wait()
        for copy in scatters[g]:
            copy.wait_recv()
        total = own[g, own_rows, :]
        for i in range(3):
            total = total + orecv[g, i].astype(F32)
        old = hid[pl.ds(pl.multiple_of(base[g] + col * block, block), block), :].astype(F32)
        resid[g, own_rows, :] = (old + total).astype(BF16)
        spreads[g] = [start(remote(resid.at[g, own_rows], resid.at[g, own_rows], ag_sem.at[0, g, i], ag_sem.at[1, g, i],
                                   {'col': zpeers[i]})) for i in (1, 2, 0)]

    stage1, stage2, act_y, act_c, act_w = {}, {}, {}, {}, {}

    def norm(g):
        for copy in spreads[g]:
            copy.wait_recv()
        resid_p[g, 0:rows, :] = resid[g, mine, :]
        resid_p[g, rows:, :] = resid[g, theirs, :]
        res = resid_p[g].astype(F32)
        sq_sum = jnp.sum(res * res, axis=1, keepdims=True)
        z_p[g] = (res * (local_scale(sq_sum, width) * DOWNSCALE) * g_ref[...].astype(F32).reshape(1, -1)).astype(BF16)
        wide = jnp.broadcast_to(sq_sum, (group_rows, LANES))
        sums_p[g] = wide[0:rows]
        high, low = split_square(wide[rows:])
        send1[g, n_tiles, :, 0:LANES] = high
        send1[g, n_tiles, :, LANES:] = low
        stage1[g, n_chunks] = start(remote(send1.at[g, n_tiles], recv1.at[g, n_tiles], s1_sem.at[0, g, n_chunks],
                                           s1_sem.at[1, g, n_chunks], {'row': mate}))

    def multiply(g, k):
        first, count = chunks[k]
        if g == 0:
            @pl.loop(first, first + count)
            def _(t):
                for copy in tile_loads(t):
                    copy.wait()

        @pl.loop(first, first + count, unroll=count)
        def _(t):
            prod = jnp.dot(z_p[g], wgu[t], preferred_element_type=F32)
            part[g, t] = prod[0:rows]
            send1[g, t] = prod[rows:].astype(BF16)

        at = pl.ds(first, count)
        stage1[g, k] = start(remote(send1.at[g, at], recv1.at[g, at], s1_sem.at[0, g, k], s1_sem.at[1, g, k],
                                    {'row': mate}))

    def combine(g, k):
        first, count = chunks[k]
        if k == 0:
            stage1[g, n_chunks].wait_recv()
            got = recv1[g, n_tiles].astype(F32)
            got = got[:, 0:LANES] + got[:, LANES:]
            mine_sq = sums_p[g]
            chip_sq = mine_sq + got
            chip = local_scale(chip_sq, 2 * width)
            mine_c = ratio(chip, local_scale(mine_sq, width) * DOWNSCALE)
            mate_c = ratio(chip, local_scale(got, width) * DOWNSCALE)
            for lane in range(2):
                coef[g, 0, :, lane * LANES:(lane + 1) * LANES] = mine_c
                coef[g, 1, :, lane * LANES:(lane + 1) * LANES] = mate_c
            sums_p[g] = chip_sq
            if g == 0:
                high, low = split_square(chip_sq)
                send2[n_tiles, :, 0:LANES] = high
                send2[n_tiles, :, LANES:] = low
                stage2[n_chunks] = start(remote(send2.at[n_tiles], recv2.at[n_tiles], s2_sem.at[0, n_chunks],
                                                s2_sem.at[1, n_chunks], {'row': across}))
        stage1[g, k].wait_recv()

        @pl.loop(first, first + count, unroll=2 if count % 2 == 0 else 1)
        def _(t):
            chip = part[g, t] * coef[g, 0] + recv1[g, t].astype(F32) * coef[g, 1]
            if g == 0:
                send2[t] = chip.astype(BF16)
            else:
                part[g, t] = chip

        if g == 0:
            at = pl.ds(first, count)
            stage2[k] = start(remote(send2.at[at], recv2.at[at], s2_sem.at[0, k], s2_sem.at[1, k], {'row': across}))

    def activate(k):
        first, count = chunks[k]
        if k == 0:
            stage2[n_chunks].wait_recv()
            got = recv2[n_tiles].astype(F32)
            got = got[:, 0:LANES] + got[:, LANES:]
            chip_sq = sums_p[1]
            total = local_scale(chip_sq + got, 4 * width)
            mine_c = ratio(total, local_scale(chip_sq, 2 * width))
            other_c = ratio(total, local_scale(got, 2 * width))
            for lane in range(2):
                coef[2, 0, :, lane * LANES:(lane + 1) * LANES] = mine_c
                coef[2, 1, :, lane * LANES:(lane + 1) * LANES] = other_c
        stage2[k].wait_recv()

        @pl.loop(first, first + count, unroll=2 if count % 2 == 0 else 1)
        def _(t):
            full = part[1, t] * coef[2, 0] + recv2[t].astype(F32) * coef[2, 1]
            full = full.astype(BF16).astype(F32)
            gate, up = full[:, 0:LANES], full[:, LANES:]
            acts[1, 0:rows, pl.ds(pl.multiple_of(t * LANES, LANES), LANES)] = (
                gate * (1.0 / (1.0 + jnp.exp(-gate))) * up).astype(BF16)

        at = pl.ds(first * LANES, count * LANES)
        src = acts.at[1, pl.ds(0, rows), at]
        act_y[k] = start(remote(src, acts.at[0, pl.ds(0, rows), at], ay_sem.at[0, k], ay_sem.at[1, k], {'row': across}))
        act_c[k] = start(remote(src, acts.at[1, pl.ds(rows, rows), at], ac_sem.at[0, k], ac_sem.at[1, k], {'row': mate}))

    def relay(k):
        first, count = chunks[k]
        at = pl.ds(first * LANES, count * LANES)
        act_y[k].wait_recv()
        act_w[k] = start(remote(acts.at[0, pl.ds(0, rows), at], acts.at[0, pl.ds(rows, rows), at],
                                aw_sem.at[0, k], aw_sem.at[1, k], {'row': mate}))

    def down(g, k):
        first, count = chunks[k]
        if g == 1:
            act_c[k].wait_recv()
            wd_copies[k].wait()
        else:
            act_w[k].wait_recv()
        at = pl.ds(first * LANES, count * LANES)
        prod = jnp.dot(acts[g, :, at], wd[at, :], preferred_element_type=F32)
        acc[g] = prod if k == 0 else acc[g] + prod

    down_scatter, down_spread = {}, {}

    def scatter_down(g):
        dsend[g] = acc[g].astype(BF16)
        down_scatter[g] = [start(remote(dsend.at[g, pl.ds(pl.multiple_of(zpeers[i] * block, block), block)],
                                        drecv.at[g, i], ds_sem.at[0, g, i], ds_sem.at[1, g, i], {'col': zpeers[i]}))
                           for i in (1, 2, 0)]

    def spread_down(g):
        for copy in down_scatter[g]:
            copy.wait_recv()
        total = acc[g, own_rows, :] + resid_p[g, own_rows, :].astype(F32)
        for i in range(3):
            total = total + drecv[g, i].astype(F32)
        final[g, own_rows, :] = total.astype(BF16)
        down_spread[g] = [start(remote(final.at[g, own_rows], final.at[g, own_rows], da_sem.at[0, g, i],
                                       da_sem.at[1, g, i], {'col': zpeers[i]})) for i in (1, 2, 0)]

    def finish(g):
        for copy in down_spread[g]:
            copy.wait_recv()
        for i, half in enumerate((core, 1 - core)):
            out_ref[pl.ds(pl.multiple_of(base[g] + half * rows, rows), rows), :] = final[g, i * rows:(i + 1) * rows, :]

    plan = [(project, 0), (project, 1), (spread, 0), (spread, 1), (norm, 0)]
    for k in range(n_chunks):
        plan += [(multiply, 0, k)] + ([(combine, 0, k - 1)] if k else [])
    plan += [(combine, 0, last), (norm, 1)]
    for k in range(n_chunks):
        plan += [(multiply, 1, k)] + ([(combine, 1, k - 1)] if k else [])
        if k >= EARLY:
            plan += [(activate, k - EARLY)]
    plan += [(combine, 1, last)]
    done = 0
    for k in range(n_chunks - EARLY, n_chunks):
        plan += [(activate, k)]
        while done < k:
            plan += [(down, 1, done)]
            done += 1
    plan += [(down, 1, last), (scatter_down, 1)]
    for k in range(n_chunks):
        plan += [(relay, k)] + ([(down, 0, k - 1)] if k else [])
        if k == SPREAD_AT:
            plan += [(spread_down, 1)]
    plan += [(down, 0, last), (scatter_down, 0), (finish, 1), (spread_down, 0), (finish, 0)]
    for step, *where in plan:
        step(*where)
    for copy in started:
        copy.wait_send()


def solution(mesh):
    cache_spec = P(('dp', 'row'), None, 'col', None)
    in_specs = (P('dp', 'row'), P(None, ('dp', 'row')), P(('dp', 'row')), cache_spec, cache_spec,
                P('row'), P('row', 'col'), P('col'), P('col', 'row'), P('row'),
                P('row', 'col'), P('row', 'col'), P('col', 'row'))
    out_specs = (P('dp', 'row'), cache_spec, cache_spec)
    vmem = pl.BlockSpec(memory_space=pltpu.VMEM)
    smem = pl.BlockSpec(memory_space=pltpu.SMEM)
    hbm = pl.BlockSpec(memory_space=pl.ANY)
    dma = pltpu.SemaphoreType.DMA
    pair = np.arange(HEAD_DIM) % (HEAD_DIM // 2)
    freq = (1.0 / (ROPE_THETA ** (pair.astype(np.float64) * 2.0 / HEAD_DIM))).astype(np.float32)[None, :]

    def local_layer(hidden, mrope_ids, cache_lens, k_cache, v_cache, norm_attn, w_qkv, b_qkv, w_out, norm_mlp, w_gate, w_up, w_down):
        batch, width = hidden.shape
        rows, slots, _, _ = k_cache.shape
        cols = w_qkv.shape[1]
        ff = w_gate.shape[1]
        heads = cols // HEAD_DIM - 2
        (k_flat, v_flat, hidden, w_qkv, w_out, w_gate, w_up, w_down, norm_attn, b_qkv, mrope_ids, norm_mlp, freqs) = (
            pltpu.with_memory_space_constraint(value, pltpu.HBM)
            for value in (k_cache.reshape(rows, slots, HEAD_DIM), v_cache.reshape(rows, slots, HEAD_DIM),
                          hidden, w_qkv, w_out, w_gate, w_up, w_down, norm_attn, b_qkv, mrope_ids, norm_mlp, jnp.asarray(freq)))
        cache_shape = (rows, slots, HEAD_DIM)
        query, new_key, new_val, k_near, v_near = pl.pallas_call(
            qkv_kernel, name='qkv',
            out_shape=(pltpu.VMEM((rows * 8, HEAD_DIM), F32), pltpu.VMEM((rows, HEAD_DIM), F32), pltpu.VMEM((rows, HEAD_DIM), F32),
                       pltpu.VMEM(cache_shape, BF16), pltpu.VMEM(cache_shape, BF16)),
            in_specs=[hbm] * 8, out_specs=(vmem,) * 5,
            scratch_shapes=[pltpu.VMEM((batch, width), BF16), pltpu.VMEM(norm_attn.shape, BF16), pltpu.VMEM(w_qkv.shape, BF16),
                            pltpu.VMEM(b_qkv.shape, BF16), pltpu.VMEM(mrope_ids.shape, jnp.int32), pltpu.VMEM(freq.shape, F32),
                            pltpu.VMEM((batch, cols + LANES), F32), pltpu.VMEM((batch, cols + 2 * LANES), BF16),
                            pltpu.VMEM((3, rows, cols + 2 * LANES), BF16), pltpu.VMEM((LANES, LANES), F32),
                            pltpu.VMEM((rows * 8, HEAD_DIM), F32), dma((3,)), dma((3,)), dma((6,)), dma((2, CACHE_PARTS))],
            compiler_params=pltpu.CompilerParams(collective_id=0, has_side_effects=True, vmem_limit_bytes=12 << 20),
        )(hidden, norm_attn, w_qkv, b_qkv, mrope_ids, freqs, k_flat, v_flat)

        attn, k_next, v_next = pl.pallas_call(
            functools.partial(attention_kernel, heads, UNROLL), name='attend',
            out_shape=(pltpu.VMEM((rows, heads * HEAD_DIM), BF16),
                       jax.ShapeDtypeStruct(cache_shape, BF16), jax.ShapeDtypeStruct(cache_shape, BF16)),
            in_specs=[smem, vmem, vmem, vmem, vmem, vmem], out_specs=(vmem, hbm, hbm),
            scratch_shapes=[pltpu.VMEM((rows, 16, HEAD_DIM), BF16), pltpu.VMEM((rows, 16, HEAD_DIM), BF16),
                            pltpu.VMEM((rows * 8, HEAD_DIM), F32), pltpu.VMEM((UNROLL * 8, slots), F32),
                            dma((2, rows // UNROLL)), dma((2, rows))],
            compiler_params=pltpu.CompilerParams(vmem_limit_bytes=8 << 20),
        )(cache_lens, query, new_key, new_val, k_near, v_near)

        n_tiles = ff // LANES
        chunks = [(sum(CHUNKS[:i]), count) for i, count in enumerate(CHUNKS)]
        n_chunks = len(chunks)
        gr = batch // GROUPS
        half, block = gr // 2, gr // 4
        hidden_out = pl.pallas_call(
            functools.partial(mlp_kernel, chunks), name='mlp',
            out_shape=pltpu.VMEM((batch, width), BF16),
            in_specs=[vmem] + [hbm] * 6, out_specs=vmem,
            scratch_shapes=[
                pltpu.VMEM((batch, width), BF16), pltpu.VMEM(norm_mlp.shape, BF16),
                pltpu.VMEM(w_out.shape, BF16), pltpu.VMEM((n_tiles, width, 2 * LANES), BF16), pltpu.VMEM(w_down.shape, BF16),
                pltpu.VMEM((GROUPS, gr, w_out.shape[0]), BF16), pltpu.VMEM((GROUPS, gr, width), BF16),
                pltpu.VMEM((GROUPS, 3, block, width), BF16), pltpu.VMEM((GROUPS, gr, width), F32),
                pltpu.VMEM((GROUPS, gr, width), BF16), pltpu.VMEM((GROUPS, gr, width), BF16),
                pltpu.VMEM((GROUPS, gr, width), BF16), pltpu.VMEM((GROUPS, half, LANES), F32),
                pltpu.VMEM((GROUPS + 1, 2, half, 2 * LANES), F32),
                pltpu.VMEM((GROUPS, n_tiles, half, 2 * LANES), F32),
                pltpu.VMEM((GROUPS, n_tiles + 1, half, 2 * LANES), BF16),
                pltpu.VMEM((GROUPS, n_tiles + 1, half, 2 * LANES), BF16),
                pltpu.VMEM((n_tiles + 1, half, 2 * LANES), BF16), pltpu.VMEM((n_tiles + 1, half, 2 * LANES), BF16),
                pltpu.VMEM((GROUPS, gr, ff), BF16), pltpu.VMEM((GROUPS, gr, width), F32),
                pltpu.VMEM((GROUPS, gr, width), BF16), pltpu.VMEM((GROUPS, 3, block, width), BF16),
                pltpu.VMEM((GROUPS, gr, width), BF16),
                dma, dma, dma, dma((2, n_tiles)), dma((n_chunks,)), dma((2, 3)), dma((2, GROUPS, 3)), dma((2, GROUPS, 3)),
                dma((2, GROUPS, n_chunks + 1)), dma((2, n_chunks + 1)), dma((2, n_chunks)),
                dma((2, n_chunks)), dma((2, n_chunks)), dma((2, GROUPS, 3)), dma((2, GROUPS, 3))],
            compiler_params=pltpu.CompilerParams(collective_id=1, has_side_effects=True, vmem_limit_bytes=40 << 20),
        )(attn, hidden, norm_mlp, w_out, w_gate, w_up, w_down)
        shape = (rows, slots, 1, HEAD_DIM)
        return hidden_out, k_next.reshape(shape), v_next.reshape(shape)

    return jax.shard_map(local_layer, mesh=mesh, in_specs=in_specs, out_specs=out_specs, check_vma=False)
```

profile of v0, /device:TPU:0, one launch (start us, length us, event | category | flops | bytes accessed | tf_op | source)
XLA Modules:
  0.0 70.5 jit_solution(12857410233434630838)
XLA Ops:
  0.6 0.0 copy-start
  0.6 10.4 %qkv.1 = (f32[256,128]{1,0:T(8,128)S(1)}, f32[32,128]{1,0:T(8,128)S(1)}, f32[32,128]{1,0:T(8,128)S(1)}, bf16[32,1024,128]{2,1,0:T(8,128)(2,1)S(1)}, bf16[32,1024,128]{2,1,0:T(8,128)(2,1)S(1)}) custom-call(bf16[128,896]{1,0:T(8,128)(2,1)} %h_hbm.3, bf16[896]{0:T(1024)(128)(2,1)} %g_hbm.2, bf16[896,1152]{1,0:T(8,128)(2,1)} %w_hbm.1, bf16[1152]{0:T(1024)(128)(2,1)} %b_hbm.1, ...), custom_call_target="tpu_custom_call" | custom-call | tf_op jit(solution)/shard_map/qkv/pallas_call | solution.py:491
  11.0 0.0 copy-done
  11.1 7.7 %attend.1 = (bf16[32,896]{1,0:T(8,128)(2,1)S(1)}, bf16[32,1024,128]{2,1,0:T(8,128)(2,1)}, bf16[32,1024,128]{2,1,0:T(8,128)(2,1)}) custom-call(s32[32]{0:T(128)S(1)} %copy-done, f32[256,128]{1,0:T(8,128)S(1)} %get-tuple-element.11.q_ref, f32[32,128]{1,0:T(8,128)S(1)} %get-tuple-element.12.nk_ref, f32[32,128]{1,0:T(8,128)S(1)} %get-tuple-element.13.nv_ref, ...), custom_call_target="tpu_custom_call" | custom-call | tf_op jit(solution)/shard_map/attend/pallas_call | solution.py:504
  18.7 51.1 %mlp.1 = bf16[128,896]{1,0:T(8,128)(2,1)S(1)} custom-call(bf16[32,896]{1,0:T(8,128)(2,1)S(1)} %get-tuple-element.16.o_ref, bf16[128,896]{1,0:T(8,128)(2,1)} %h_hbm.3, bf16[896]{0:T(1024)(128)(2,1)} %g_hbm.3, bf16[896,896]{1,0:T(8,128)(2,1)} %wo_hbm.1, bf16[896,4736]{1,0:T(8,128)(2,1)} %wg_hbm.1, bf16[896,4736]{1,0:T(8,128)(2,1)} %wu_hbm.1, ...), custom_call_target="tpu_custom_call" | custom-call | tf_op jit(solution)/shard_map/mlp/pallas_call | solution.py:520
  69.9 0.7 copy.20
Async XLA Ops:
  0.6 10.4 %copy-start = (s32[32]{0:T(128)S(1)}, s32[32]{0:T(128)}, u32[]{:S(2)}) copy-start(s32[32]{0:T(128)} %lens_ref.1) | copy-start | bytes 388
where the time goes:
time: 70.7 us; the launch traced here: 70.5 us
  Pallas kernels  69.2 us (98%)
    pallas_call x1, Pallas kernels, local_layer(): pl.pallas_call(functools.partial(mlp_kernel, chunks), name='mlp', out_sha...  51.1 us
    pallas_call x1, Pallas kernels, local_layer(): pl.pallas_call(qkv_kernel, name='qkv', out_shape=(pltpu.VMEM((rows * 8, H...  10.4 us
    pallas_call x1, Pallas kernels, local_layer(): pl.pallas_call(functools.partial(attention_kernel, heads, UNROLL), name='...  7.68 us

commit v1 on v0

--- a/solution.py
+++ b/solution.py
@@ -17,10 +17,11 @@
 BIG = 3.3e38
 GROUPS = 2
 UNROLL = 8
+PIECE = 512
 CACHE_PARTS = 8
-CHUNKS = (4, 8, 8, 8, 6, 3)
-EARLY = 3
-SPREAD_AT = 3
+CHUNKS = (2, 5, 8, 8, 8, 4, 2)
+EARLY = 4
+SPREAD_AT = 4
 F32 = jnp.float32
 BF16 = jnp.bfloat16
 
@@ -87,20 +88,23 @@
     scale = local_scale(sq_sum, width) * DOWNSCALE
     normed = (hid * scale * g_ref[...].astype(F32).reshape(1, -1)).astype(BF16)
     loads[2].wait()
-    prod = jnp.dot(normed, w_ref[...], preferred_element_type=F32)
-    part[:, 0:cols] = prod
     wide = jnp.broadcast_to(sq_sum, (hid.shape[0], LANES))
     part[:, cols:] = wide
-    send[:, 0:cols] = prod.astype(BF16)
     high, low = split_square(wide)
-    send[:, cols:cols + LANES] = high
-    send[:, cols + LANES:] = low
-    pl.semaphore_wait(barrier, 3)
+    lane = lax.broadcasted_iota(jnp.int32, wide.shape, 1)
+    send[:, 0:LANES] = jnp.where(lane < LANES // 2, high.astype(F32), low.astype(F32)).astype(BF16)
     copies = []
-    for slot in (2, 1, 0):
-        copies.append(remote(send.at[pl.ds(pl.multiple_of(peers[slot] * rows, rows), rows)], recv.at[slot],
-                             send_sem.at[slot], recv_sem.at[slot], {'row': peers[slot]}))
-        copies[-1].start()
+    for piece, (lo, hi) in enumerate(((0, PIECE), (PIECE, cols))):
+        prod = jnp.dot(normed, w_ref[:, lo:hi], preferred_element_type=F32)
+        part[:, lo:hi] = prod
+        send[:, LANES + lo:LANES + hi] = prod.astype(BF16)
+        if piece == 0:
+            pl.semaphore_wait(barrier, 3)
+        at = pl.ds(0, LANES + hi) if piece == 0 else pl.ds(LANES + lo, hi - lo)
+        for slot in (2, 1, 0):
+            copies.append(remote(send.at[pl.ds(pl.multiple_of(peers[slot] * rows, rows), rows), at], recv.at[slot, :, at],
+                                 send_sem.at[piece, slot], recv_sem.at[piece, slot], {'row': peers[slot]}))
+            copies[-1].start()
 
     for copy in loads[3:]:
         copy.wait()
@@ -119,8 +123,8 @@
     parts = [mine[:, 0:cols]]
     for slot in range(3):
         block = recv[slot].astype(F32)
-        sums.append(block[:, cols:cols + 1] + block[:, cols + LANES:cols + LANES + 1])
-        parts.append(block[:, 0:cols])
+        sums.append(block[:, 0:1] + block[:, LANES // 2:LANES // 2 + 1])
+        parts.append(block[:, LANES:])
     total = local_scale(sums[0] + sums[1] + sums[2] + sums[3], 4 * width)
     qkv = jnp.zeros((rows, cols), F32)
     for square, block in zip(sums, parts):
@@ -139,8 +143,8 @@
         copy.wait()
 
 
-def attention_kernel(group, unroll, lens_ref, q_ref, nk_ref, nv_ref, k_ref, v_ref, o_ref, k_out, v_out,
-                     k_patch, v_patch, o_rows, s_buf, out_sem, patch_sem):
+def attention_kernel(group, unroll, lens_ref, q_ref, nk_ref, nv_ref, k_in, v_in, o_ref, k_out, v_out, k_ref, v_ref,
+                     o_rows, s_buf, out_sem):
     rows, slots = k_ref.shape[0], k_ref.shape[1]
     steps = rows // unroll
 
@@ -149,22 +153,18 @@
         return (pltpu.make_async_copy(k_ref.at[at], k_out.at[at], out_sem.at[0, step]),
                 pltpu.make_async_copy(v_ref.at[at], v_out.at[at], out_sem.at[1, step]))
 
-    def patches(b):
-        base = pl.multiple_of((lens_ref[b] // 16) * 16, 16)
-        return (pltpu.make_async_copy(k_patch.at[b], k_out.at[b, pl.ds(base, 16)], patch_sem.at[0, b]),
-                pltpu.make_async_copy(v_patch.at[b], v_out.at[b, pl.ds(base, 16)], patch_sem.at[1, b]))
-
     for step in range(steps):
-        for copy in stores(step):
-            copy.start()
-
-    @pl.loop(0, rows)
-    def _(b):
-        base = pl.multiple_of((lens_ref[b] // 16) * 16, 16)
-        hit = lax.broadcasted_iota(jnp.int32, (16, HEAD_DIM), 0) == lens_ref[b] % 16
-        for src, new, patch in ((k_ref, nk_ref, k_patch), (v_ref, nv_ref, v_patch)):
-            old = src[b, pl.ds(base, 16), :].astype(F32)
-            patch[b] = jnp.where(hit, new[pl.ds(b, 1), :], old).astype(BF16)
+        for b in range(step * unroll, (step + 1) * unroll):
+            base = pl.multiple_of((lens_ref[b] // 16) * 16, 16)
+            hit = lax.broadcasted_iota(jnp.int32, (16, HEAD_DIM), 0) == lens_ref[b] % 16
+            for cache, new in ((k_ref, nk_ref), (v_ref, nv_ref)):
+                old = cache[b, pl.ds(base, 16), :].astype(F32)
+                cache[b, pl.ds(base, 16), :] = jnp.where(hit, new[b:b + 1, :], old).astype(BF16)
+        if step:
+            for copy in stores(step - 1):
+                copy.start()
+    for copy in stores(steps - 1):
+        copy.start()
 
     @pl.loop(0, steps)
     def _(step):
@@ -172,37 +172,20 @@
         position = lax.broadcasted_iota(jnp.int32, (8, slots), 1)
         for u, b in enumerate(items):
             query = q_ref[pl.ds(pl.multiple_of(b * 8, 8), 8), :]
-            scores = lax.dot_general(query.astype(BF16), k_ref[b], (((1,), (1,)), ((), ())), preferred_element_type=F32)
-            fresh = jnp.sum(query * nk_ref[pl.ds(b, 1), :], axis=1, keepdims=True)
-            scores = jnp.where(position == lens_ref[b], fresh, scores) * (HEAD_DIM ** -0.5)
+            scores = lax.dot_general(query.astype(BF16), k_ref[b], (((1,), (1,)), ((), ())),
+                                     preferred_element_type=F32) * (HEAD_DIM ** -0.5)
             s_buf[u * 8:(u + 1) * 8, :] = jnp.where(position <= lens_ref[b], scores, -1e30)
         scores = s_buf[...]
         weight = jnp.exp(scores - jnp.max(scores, axis=1, keepdims=True))
         s_buf[...] = weight / jnp.sum(weight, axis=1, keepdims=True)
         for u, b in enumerate(items):
             prob = s_buf[u * 8:(u + 1) * 8, :].astype(BF16)
-            newest = position == lens_ref[b]
-            prob_f = prob.astype(F32)
-            fresh = jnp.sum(jnp.where(newest, prob_f, 0.0), axis=1, keepdims=True)
-            rest = jnp.where(newest, 0.0, prob_f).astype(BF16)
-            o_rows[pl.ds(pl.multiple_of(b * 8, 8), 8), :] = (
-                jnp.dot(rest, v_ref[b], preferred_element_type=F32) + fresh * nv_ref[pl.ds(b, 1), :])
+            o_rows[pl.ds(pl.multiple_of(b * 8, 8), 8), :] = jnp.dot(prob, v_ref[b], preferred_element_type=F32)
 
     for head in range(group):
         o_ref[:, head * HEAD_DIM:(head + 1) * HEAD_DIM] = o_rows[pl.ds(head, rows, stride=8), :].astype(BF16)
-
     for step in range(steps):
         for copy in stores(step):
-            copy.wait()
-
-        @pl.loop(step * unroll, (step + 1) * unroll)
-        def _(b):
-            for copy in patches(b):
-                copy.start()
-
-    @pl.loop(0, rows)
-    def _(b):
-        for copy in patches(b):
             copy.wait()
 
 
@@ -437,9 +420,11 @@
         for i, half in enumerate((core, 1 - core)):
             out_ref[pl.ds(pl.multiple_of(base[g] + half * rows, rows), rows), :] = final[g, i * rows:(i + 1) * rows, :]
 
-    plan = [(project, 0), (project, 1), (spread, 0), (spread, 1), (norm, 0)]
+    plan = [(project, 0), (spread, 0), (project, 1), (norm, 0)]
     for k in range(n_chunks):
         plan += [(multiply, 0, k)] + ([(combine, 0, k - 1)] if k else [])
+        if k == 1:
+            plan += [(spread, 1)]
     plan += [(combine, 0, last), (norm, 1)]
     for k in range(n_chunks):
         plan += [(multiply, 1, k)] + ([(combine, 1, k - 1)] if k else [])
@@ -495,20 +480,20 @@
             in_specs=[hbm] * 8, out_specs=(vmem,) * 5,
             scratch_shapes=[pltpu.VMEM((batch, width), BF16), pltpu.VMEM(norm_attn.shape, BF16), pltpu.VMEM(w_qkv.shape, BF16),
                             pltpu.VMEM(b_qkv.shape, BF16), pltpu.VMEM(mrope_ids.shape, jnp.int32), pltpu.VMEM(freq.shape, F32),
-                            pltpu.VMEM((batch, cols + LANES), F32), pltpu.VMEM((batch, cols + 2 * LANES), BF16),
-                            pltpu.VMEM((3, rows, cols + 2 * LANES), BF16), pltpu.VMEM((LANES, LANES), F32),
-                            pltpu.VMEM((rows * 8, HEAD_DIM), F32), dma((3,)), dma((3,)), dma((6,)), dma((2, CACHE_PARTS))],
+                            pltpu.VMEM((batch, cols + LANES), F32), pltpu.VMEM((batch, cols + LANES), BF16),
+                            pltpu.VMEM((3, rows, cols + LANES), BF16), pltpu.VMEM((LANES, LANES), F32),
+                            pltpu.VMEM((rows * 8, HEAD_DIM), F32), dma((2, 3)), dma((2, 3)), dma((6,)), dma((2, CACHE_PARTS))],
             compiler_params=pltpu.CompilerParams(collective_id=0, has_side_effects=True, vmem_limit_bytes=12 << 20),
         )(hidden, norm_attn, w_qkv, b_qkv, mrope_ids, freqs, k_flat, v_flat)
 
-        attn, k_next, v_next = pl.pallas_call(
+        attn, k_next, v_next, _, _ = pl.pallas_call(
             functools.partial(attention_kernel, heads, UNROLL), name='attend',
             out_shape=(pltpu.VMEM((rows, heads * HEAD_DIM), BF16),
-                       jax.ShapeDtypeStruct(cache_shape, BF16), jax.ShapeDtypeStruct(cache_shape, BF16)),
-            in_specs=[smem, vmem, vmem, vmem, vmem, vmem], out_specs=(vmem, hbm, hbm),
-            scratch_shapes=[pltpu.VMEM((rows, 16, HEAD_DIM), BF16), pltpu.VMEM((rows, 16, HEAD_DIM), BF16),
-                            pltpu.VMEM((rows * 8, HEAD_DIM), F32), pltpu.VMEM((UNROLL * 8, slots), F32),
-                            dma((2, rows // UNROLL)), dma((2, rows))],
+                       jax.ShapeDtypeStruct(cache_shape, BF16), jax.ShapeDtypeStruct(cache_shape, BF16),
+                       pltpu.VMEM(cache_shape, BF16), pltpu.VMEM(cache_shape, BF16)),
+            in_specs=[smem, vmem, vmem, vmem, vmem, vmem], out_specs=(vmem, hbm, hbm, vmem, vmem),
+            input_output_aliases={4: 3, 5: 4},
+            scratch_shapes=[pltpu.VMEM((rows * 8, HEAD_DIM), F32), pltpu.VMEM((UNROLL * 8, slots), F32), dma((2, rows // UNROLL))],
             compiler_params=pltpu.CompilerParams(vmem_limit_bytes=8 << 20),
         )(cache_lens, query, new_key, new_val, k_near, v_near)
 

time: 70.7 us -> 68.1 us (0.963)
  Pallas kernels: 69.2 us -> 66.6 us
    pallas_call x1, Pallas kernels: 7.68 us -> 6.58 us  [local_layer(): pl.pallas_call(functools.partial(attention_kernel, heads, UNROLL), name='...]
    pallas_call x1, Pallas kernels: 51.1 us -> 50.1 us  [local_layer(): pl.pallas_call(functools.partial(mlp_kernel, chunks), name='mlp', out_sha...]
where the time goes in v1:
time: 68.1 us; the launch traced here: 68 us
  Pallas kernels  66.6 us (98%)
  local copies, waits for them, and re-layouts  0.69 us (1%)
    pallas_call x1, Pallas kernels, local_layer(): pl.pallas_call(functools.partial(mlp_kernel, chunks), name='mlp', out_sha...  50.1 us
    pallas_call x1, Pallas kernels, local_layer(): pl.pallas_call(qkv_kernel, name='qkv', out_shape=(pltpu.VMEM((rows * 8, H...  9.95 us
    pallas_call x1, Pallas kernels, local_layer(): pl.pallas_call(functools.partial(attention_kernel, heads, UNROLL), name='...  6.58 us

profile of v1, /device:TPU:0, one launch (start us, length us, event | category | flops | bytes accessed | tf_op | source)
XLA Modules:
  0.0 68.0 jit_solution(15309935991761832659)
XLA Ops:
  0.6 0.0 copy-start
  0.6 9.9 %qkv.1 = (f32[256,128]{1,0:T(8,128)S(1)}, f32[32,128]{1,0:T(8,128)S(1)}, f32[32,128]{1,0:T(8,128)S(1)}, bf16[32,1024,128]{2,1,0:T(8,128)(2,1)S(1)}, bf16[32,1024,128]{2,1,0:T(8,128)(2,1)S(1)}) custom-call(bf16[128,896]{1,0:T(8,128)(2,1)} %h_hbm.3, bf16[896]{0:T(1024)(128)(2,1)} %g_hbm.2, bf16[896,1152]{1,0:T(8,128)(2,1)} %w_hbm.1, bf16[1152]{0:T(1024)(128)(2,1)} %b_hbm.1, ...), custom_call_target="tpu_custom_call" | custom-call | tf_op jit(solution)/shard_map/qkv/pallas_call | solution.py:476
  10.6 0.0 copy-done
  10.6 6.6 %attend.1 = (bf16[32,896]{1,0:T(8,128)(2,1)S(1)}, bf16[32,1024,128]{2,1,0:T(8,128)(2,1)}, bf16[32,1024,128]{2,1,0:T(8,128)(2,1)}, bf16[32,1024,128]{2,1,0:T(8,128)(2,1)S(1)}, bf16[32,1024,128]{2,1,0:T(8,128)(2,1)S(1)}) custom-call(s32[32]{0:T(128)S(1)} %copy-done, ...), custom_call_target="tpu_custom_call", output_to_operand_aliasing={{3}: (4, {}), {4}: (5, {})} | custom-call | tf_op jit(solution)/shard_map/attend/pallas_call | solution.py:489
  17.2 50.1 %mlp.1 = bf16[128,896]{1,0:T(8,128)(2,1)S(1)} custom-call(bf16[32,896]{1,0:T(8,128)(2,1)S(1)} %get-tuple-element.16.o_ref, bf16[128,896]{1,0:T(8,128)(2,1)} %h_hbm.3, bf16[896]{0:T(1024)(128)(2,1)} %g_hbm.3, bf16[896,896]{1,0:T(8,128)(2,1)} %wo_hbm.1, bf16[896,4736]{1,0:T(8,128)(2,1)} %wg_hbm.1, bf16[896,4736]{1,0:T(8,128)(2,1)} %wu_hbm.1, ...), custom_call_target="tpu_custom_call" | custom-call | tf_op jit(solution)/shard_map/mlp/pallas_call | solution.py:505
  67.3 0.7 %copy.24 = bf16[128,896]{1,0:T(8,128)(2,1)} copy(bf16[128,896]{1,0:T(8,128)(2,1)S(1)} %mlp.1) | data formatting | bytes 458752
Async XLA Ops:
  0.6 10.0 %copy-start = (s32[32]{0:T(128)S(1)}, s32[32]{0:T(128)}, u32[]{:S(2)}) copy-start(s32[32]{0:T(128)} %lens_ref.1) | copy-start | bytes 388

commit v2 on v1

--- a/solution.py
+++ b/solution.py
@@ -19,9 +19,9 @@
 UNROLL = 8
 PIECE = 512
 CACHE_PARTS = 8
-CHUNKS = (2, 5, 8, 8, 8, 4, 2)
-EARLY = 4
-SPREAD_AT = 4
+CHUNKS = (4, 8, 8, 8, 6, 3)
+EARLY = 3
+SPREAD_AT = 3
 F32 = jnp.float32
 BF16 = jnp.bfloat16
 
@@ -197,6 +197,8 @@
     core, y = row % 2, row // 2
     col = lax.axis_index('col')
     zpeers = [(col + step) % 4 for step in (1, 2, 3)]
+    far = [3 - 3 * (col // 2), 2 - col // 2, col + 1 - 2 * (col % 2)]
+    slots = [(peer - col + 4) % 4 - 1 for peer in far]
     n_tiles = wgu.shape[0]
     width = hid.shape[1]
     group_rows = resid.shape[1]
@@ -400,9 +402,9 @@
 
     def scatter_down(g):
         dsend[g] = acc[g].astype(BF16)
-        down_scatter[g] = [start(remote(dsend.at[g, pl.ds(pl.multiple_of(zpeers[i] * block, block), block)],
-                                        drecv.at[g, i], ds_sem.at[0, g, i], ds_sem.at[1, g, i], {'col': zpeers[i]}))
-                           for i in (1, 2, 0)]
+        down_scatter[g] = [start(remote(dsend.at[g, pl.ds(pl.multiple_of(far[i] * block, block), block)],
+                                        drecv.at[g, slots[i]], ds_sem.at[0, g, i], ds_sem.at[1, g, slots[i]], {'col': far[i]}))
+                           for i in range(3)]
 
     def spread_down(g):
         for copy in down_scatter[g]:
@@ -412,7 +414,7 @@
             total = total + drecv[g, i].astype(F32)
         final[g, own_rows, :] = total.astype(BF16)
         down_spread[g] = [start(remote(final.at[g, own_rows], final.at[g, own_rows], da_sem.at[0, g, i],
-                                       da_sem.at[1, g, i], {'col': zpeers[i]})) for i in (1, 2, 0)]
+                                       da_sem.at[1, g, slots[i]], {'col': far[i]})) for i in range(3)]
 
     def finish(g):
         for copy in down_spread[g]:
@@ -423,7 +425,7 @@
     plan = [(project, 0), (spread, 0), (project, 1), (norm, 0)]
     for k in range(n_chunks):
         plan += [(multiply, 0, k)] + ([(combine, 0, k - 1)] if k else [])
-        if k == 1:
+        if k == 2:
             plan += [(spread, 1)]
     plan += [(combine, 0, last), (norm, 1)]
     for k in range(n_chunks):

time: 68.1 us -> 67.8 us (level)
  no operation moved by 1% of the time
where the time goes in v2:
time: 67.8 us; the launch traced here: 67.7 us
  Pallas kernels  66.3 us (98%)
  local copies, waits for them, and re-layouts  0.69 us (1%)
    pallas_call x1, Pallas kernels, local_layer(): pl.pallas_call(functools.partial(mlp_kernel, chunks), name='mlp', out_sha...  49.8 us
    pallas_call x1, Pallas kernels, local_layer(): pl.pallas_call(qkv_kernel, name='qkv', out_shape=(pltpu.VMEM((rows * 8, H...  9.95 us
    pallas_call x1, Pallas kernels, local_layer(): pl.pallas_call(functools.partial(attention_kernel, heads, UNROLL), name='...  6.58 us

profile of v2, /device:TPU:0, one launch (start us, length us, event | category | flops | bytes accessed | tf_op | source)
XLA Modules:
  0.0 67.7 jit_solution(7409703397556016778)
XLA Ops:
  0.6 0.0 copy-start
  0.6 9.9 %qkv.1 = (f32[256,128]{1,0:T(8,128)S(1)}, f32[32,128]{1,0:T(8,128)S(1)}, f32[32,128]{1,0:T(8,128)S(1)}, bf16[32,1024,128]{2,1,0:T(8,128)(2,1)S(1)}, bf16[32,1024,128]{2,1,0:T(8,128)(2,1)S(1)}) custom-call(bf16[128,896]{1,0:T(8,128)(2,1)} %h_hbm.3, bf16[896]{0:T(1024)(128)(2,1)} %g_hbm.2, bf16[896,1152]{1,0:T(8,128)(2,1)} %w_hbm.1, bf16[1152]{0:T(1024)(128)(2,1)} %b_hbm.1, ...), custom_call_target="tpu_custom_call" | custom-call | tf_op jit(solution)/shard_map/qkv/pallas_call | solution.py:478
  10.6 0.0 copy-done
  10.6 6.6 %attend.1 = (bf16[32,896]{1,0:T(8,128)(2,1)S(1)}, bf16[32,1024,128]{2,1,0:T(8,128)(2,1)}, bf16[32,1024,128]{2,1,0:T(8,128)(2,1)}, bf16[32,1024,128]{2,1,0:T(8,128)(2,1)S(1)}, bf16[32,1024,128]{2,1,0:T(8,128)(2,1)S(1)}) custom-call(s32[32]{0:T(128)S(1)} %copy-done, ...), custom_call_target="tpu_custom_call", output_to_operand_aliasing={{3}: (4, {}), {4}: (5, {})} | custom-call | tf_op jit(solution)/shard_map/attend/pallas_call | solution.py:491
  17.2 49.8 %mlp.1 = bf16[128,896]{1,0:T(8,128)(2,1)S(1)} custom-call(bf16[32,896]{1,0:T(8,128)(2,1)S(1)} %get-tuple-element.16.o_ref, bf16[128,896]{1,0:T(8,128)(2,1)} %h_hbm.3, bf16[896]{0:T(1024)(128)(2,1)} %g_hbm.3, bf16[896,896]{1,0:T(8,128)(2,1)} %wo_hbm.1, bf16[896,4736]{1,0:T(8,128)(2,1)} %wg_hbm.1, bf16[896,4736]{1,0:T(8,128)(2,1)} %wu_hbm.1, ...), custom_call_target="tpu_custom_call" | custom-call | tf_op jit(solution)/shard_map/mlp/pallas_call | solution.py:507
  67.0 0.7 %copy.24 = bf16[128,896]{1,0:T(8,128)(2,1)} copy(bf16[128,896]{1,0:T(8,128)(2,1)S(1)} %mlp.1) | data formatting | bytes 458752
Async XLA Ops:
  0.6 10.0 %copy-start = (s32[32]{0:T(128)S(1)}, s32[32]{0:T(128)}, u32[]{:S(2)}) copy-start(s32[32]{0:T(128)} %lens_ref.1) | copy-start | bytes 388
